TPU v7x, 16 devices: a 4x2x1 block of a 4x4x8 slice. The times are simulated.
16 devices in a mesh: rep: 2 (over y, z), dp: 8 (over x, core).
Axes of the slice: x: 4, y: 2, z: 1, core: 2. Of those that a mesh axis runs over, the one named last changes fastest.
The devices are a block of a 4x4x8 slice.
Arguments:
- x: bfloat16 [16, 2048, 768], P(('rep', 'dp')), parts along dimension 0
- dy: bfloat16 [16, 2048, 768], P(('rep', 'dp')), parts along dimension 0
- w_gate: bfloat16 [2, 768, 6144], P(None, 'dp')
- w_up: bfloat16 [2, 768, 6144], P(None, 'dp')
- w_down: bfloat16 [2, 6144, 768], P(None, 'dp')
- m_w_gate: float32 [2, 768, 6144], P(None, 'dp')
- m_w_up: float32 [2, 768, 6144], P(None, 'dp')
- m_w_down: float32 [2, 6144, 768], P(None, 'dp')
- v_w_gate: float32 [2, 768, 6144], P(None, 'dp')
- v_w_up: float32 [2, 768, 6144], P(None, 'dp')
- v_w_down: float32 [2, 6144, 768], P(None, 'dp')
Outputs:
- output 1: bfloat16 [4, 768, 6144], P('rep', 'dp'), parts along dimension 0
- output 2: bfloat16 [4, 768, 6144], P('rep', 'dp'), parts along dimension 0
- output 3: bfloat16 [4, 6144, 768], P('rep', 'dp'), parts along dimension 0
- output 4: float32 [4, 768, 6144], P('rep', 'dp'), parts along dimension 0
- output 5: float32 [4, 768, 6144], P('rep', 'dp'), parts along dimension 0
- output 6: float32 [4, 6144, 768], P('rep', 'dp'), parts along dimension 0
- output 7: float32 [4, 768, 6144], P('rep', 'dp'), parts along dimension 0
- output 8: float32 [4, 768, 6144], P('rep', 'dp'), parts along dimension 0
- output 9: float32 [4, 6144, 768], P('rep', 'dp'), parts along dimension 0
There are 2 independent parts. A program takes and returns all parts, laid end to end along the dimension named above; an argument that names none is the same for every part.
All inputs are finite; a program needn't handle non-finite values.
Results may differ from a plain program's by a relative error of at most 0.022.
Values are sent between devices in bfloat16 or wider.
A program may use at most 768 MiB of HBM per device.

v0:
```python
import functools

import jax
import jax.numpy as jnp
from jax import lax
from jax.experimental import pallas as pl
from jax.experimental.pallas import tpu as pltpu
from jax.sharding import PartitionSpec as P


BF16, F32 = jnp.bfloat16, jnp.float32
MESH = pl.DeviceIdType.MESH
NT, TN = ((1,), (1,)), ((0,), (0,))


def mm(a, w, dims):
    return lax.dot_general(a, w, (dims, ((), ())), preferred_element_type=F32)


def normed(h):
    wide = h.astype(F32)
    scale = lax.rsqrt(jnp.mean(wide**2, -1, keepdims=True) + 1e-6)
    return (wide * scale).astype(BF16)


def forward_kernel(n, x_ref, dy_ref, sg, su, sd, wg, wu, wd, keep_up, keep_gate, hid0, hid1, by_gate, by_up, h1, a1, a0, wd_v, send, recv, local, load):
    me = lax.axis_index("dp")
    chip, core = me // 2, lax.rem(me, 2)
    ring = n // 2
    at = lambda c, k: 2 * lax.rem(c, ring) + k
    right, left, partner = at(chip + 1, core), at(chip + ring - 1, core), at(chip, 1 - core)
    far = at(chip + 2, core)

    barrier = pltpu.get_barrier_semaphore()
    for other in (left, right, partner):
        pl.semaphore_signal(barrier, inc=1, device_id={"dp": other}, device_id_type=MESH)
    pl.semaphore_wait(barrier, 3)

    tokens, ff = hid0.shape
    d = x_ref.shape[1]
    third = ff // 3
    everything = (0, ff)
    units = [(sg, wg, 0, everything), (su, wu, 0, everything), (sd, wd, 0, (0, d)), (sd, wd, 1, (0, d))]
    for t in range(3):
        units += [(sg, wg, 1, (t * third, third)), (su, wu, 1, (t * third, third))]

    def span(u, part):
        depth = units[u][0].shape[1]
        half = depth // 2
        return {"all": (0, depth), "a": (0, half), "b": (half, half)}[part]

    def rows(u, owner, part):
        shard, full, layer, columns = units[u]
        start, size = span(u, part)
        return full.at[layer, pl.ds(pl.multiple_of(owner * shard.shape[1] + start, 16), size), pl.ds(*columns)]

    def own(u, part):
        shard, _, layer, columns = units[u]
        return shard.at[layer, pl.ds(*span(u, part)), pl.ds(*columns)]

    def move(u, kind):
        source, rows_of, to = [
            (own(u, "a"), (me, "a"), right),
            (own(u, "b"), (me, "b"), right),
            (own(u, "b"), (me, "b"), left),
            (own(u, "a"), (me, "a"), left),
            (None, (left, "a"), right),
            (None, (right, "b"), left),
            (own(u, "all"), (me, "all"), partner),
            (None, (left, "all"), partner),
            (None, (right, "all"), partner),
            (None, (far, "a"), partner),
            (None, (far, "b"), partner),
        ][kind]
        there = rows(u, *rows_of)
        return pltpu.make_async_remote_copy(
            src_ref=there if source is None else source,
            dst_ref=there,
            send_sem=send.at[u, kind],
            recv_sem=recv.at[u, kind],
            device_id={"dp": to},
            device_id_type=MESH,
        )

    def keep(u):
        return pltpu.make_async_copy(own(u, "all"), rows(u, me, "all"), local.at[u])

    def post(u):
        for kind in (0, 2, 1, 3, 6):
            move(u, kind).start()
        keep(u).start()

    def pass_on(arrived, onward):
        def act(u):
            for one, other in zip(arrived, onward):
                move(u, one).wait_recv()
                move(u, other).start()

        return act

    middle, relay, relay_far = pass_on((0, 2), (4, 5)), pass_on((1, 3), (7, 8)), pass_on((4, 5), (9, 10))

    def finish(u):
        for kind in (6, 7, 8, 9, 10):
            move(u, kind).wait_recv()
        keep(u).wait()

    def both(act, pair):
        act(4 + 2 * pair)
        act(5 + 2 * pair)

    bn, sub = 256, 256

    def when(step, plan):
        for number, act in plan.items():
            pl.when(step == number)(act)

    def first_layer(plan):
        def body(g_ref, u_ref, ku_ref, kg_ref, h_ref):
            when(pl.program_id(0), plan)
            for r in range(0, tokens, sub):
                here = pl.ds(r, sub)
                gate = jnp.dot(a0[here, :], g_ref[...], preferred_element_type=F32)
                up = jnp.dot(a0[here, :], u_ref[...], preferred_element_type=F32)
                sig = 0.5 * jnp.tanh(0.5 * gate) + 0.5
                silu = gate * sig
                ku_ref[here, :] = silu
                kg_ref[here, :] = up * (sig + silu * (1 - sig))
                h_ref[here, :] = (silu * up).astype(BF16)

        w, tile = pl.BlockSpec((d, bn), lambda j: (0, j)), pl.BlockSpec((tokens, bn), lambda j: (0, j))
        pltpu.emit_pipeline(body, grid=(ff // bn,), in_specs=[w, w], out_specs=[tile] * 3)(
            wg.at[0], wu.at[0], keep_up, keep_gate, hid0
        )

    def last_layer(part, plan):
        steps = third // bn

        def body(g_ref, u_ref, d_ref, h_ref, bg_ref, bu_ref):
            when(pl.program_id(0), plan)
            for r in range(0, tokens, sub):
                here = pl.ds(r, sub)
                gate = jnp.dot(a1[here, :], g_ref[...], preferred_element_type=F32)
                up = jnp.dot(a1[here, :], u_ref[...], preferred_element_type=F32)
                by = mm(dy_ref[here, :], d_ref[...], NT).astype(BF16).astype(F32)
                sig = 0.5 * jnp.tanh(0.5 * gate) + 0.5
                silu = gate * sig
                h_ref[here, :] = (silu * up).astype(BF16)
                bu_ref[here, :] = (by * silu).astype(BF16)
                bg_ref[here, :] = (by * (up * (sig + silu * (1 - sig)))).astype(BF16)

        w = pl.BlockSpec((d, bn), lambda j: (0, part * steps + j))
        wt = pl.BlockSpec((bn, d), lambda j: (part * steps + j, 0))
        tile = pl.BlockSpec((tokens, bn), lambda j: (0, part * steps + j))
        pltpu.emit_pipeline(body, grid=(steps,), in_specs=[w, w, wt], out_specs=[tile] * 3)(
            wg.at[1], wu.at[1], wd.at[1], hid1, by_gate, by_up
        )

    rm = 256

    def down(plan):
        def body(hid_ref):
            i = pl.program_id(0)
            when(i, plan)
            here = pl.ds(pl.multiple_of(i * rm, rm), rm)
            out = jnp.dot(hid_ref[...], wd_v[...], preferred_element_type=F32).astype(BF16)
            h = (x_ref[here, :].astype(F32) + out.astype(F32)).astype(BF16)
            h1[here, :] = h
            a1[here, :] = normed(h)

        pltpu.emit_pipeline(body, grid=(tokens // rm,), in_specs=[pl.BlockSpec((rm, ff), lambda i: (i, 0))], out_specs=[])(hid0)

    def run(*acts):
        def act():
            for f, u in acts:
                f(u)

        return act

    post(0)
    post(1)

    @pl.loop(0, tokens // rm)
    def _(i):
        here = pl.ds(pl.multiple_of(i * rm, rm), rm)
        a0[here, :] = normed(x_ref[here, :])

    run((middle, 0), (relay, 0), (middle, 1), (post, 2), (relay, 1), (relay_far, 0), (relay_far, 1), (post, 3), (finish, 0), (finish, 1))()
    pair = lambda p: lambda act: lambda: both(act, p)
    p0, p1, p2 = pair(0), pair(1), pair(2)
    first_layer(
        {
            6: run((middle, 2)),
            11: run((relay, 2)),
            12: p0(post),
            16: run((middle, 3)),
            21: run((relay, 3)),
        }
    )
    run((relay_far, 2), (finish, 2))()
    get = pltpu.make_async_copy(wd.at[0], wd_v, load)
    get.start()
    get.wait()

    def after_first():
        p0(middle)()
        p1(post)()

    down({3: after_first, 6: p0(relay)})
    run((relay_far, 3), (finish, 3))()
    p0(relay_far)()
    p0(finish)()

    def after_second():
        p1(middle)()
        p2(post)()

    last_layer(0, {2: after_second, 5: p1(relay)})
    p1(relay_far)()
    p1(finish)()
    last_layer(1, {2: p2(middle), 5: p2(relay)})
    p2(relay_far)()
    p2(finish)()
    last_layer(2, {})
    for u in range(len(units)):
        for kind in range(11):
            move(u, kind).wait_send()


def forward(n, x, dy, sg, su, sd):
    tokens, d = x.shape
    ff = sg.shape[-1]
    layers = sg.shape[0]
    vmem, hbm = pl.BlockSpec(memory_space=pltpu.VMEM), pl.BlockSpec(memory_space=pl.ANY)
    s = jax.ShapeDtypeStruct
    wide, thin = s((tokens, ff), F32), s((tokens, ff), BF16)
    units, kinds = 10, 11
    return pl.pallas_call(
        functools.partial(forward_kernel, n),
        out_shape=(
            s((layers, d, ff), BF16), s((layers, d, ff), BF16), s((layers, ff, d), BF16),
            wide, wide, thin, thin, thin, thin, s((tokens, d), BF16), s((tokens, d), BF16),
        ),
        in_specs=[vmem] * 5,
        out_specs=[hbm] * 9 + [vmem] * 2,
        scratch_shapes=[
            pltpu.VMEM((tokens, d), BF16),
            pltpu.VMEM((ff, d), BF16),
            pltpu.SemaphoreType.DMA((units, kinds)),
            pltpu.SemaphoreType.DMA((units, kinds)),
            pltpu.SemaphoreType.DMA((units,)),
            pltpu.SemaphoreType.DMA,
        ],
        compiler_params=pltpu.CompilerParams(collective_id=0, has_side_effects=True, vmem_limit_bytes=63 * 1024 * 1024),
        name="forward",
    )(x, dy, sg, su, sd)


def normed_back(h, by_a):
    wide, by = h.astype(F32), by_a.astype(F32)
    scale = lax.rsqrt(jnp.mean(wide**2, -1, keepdims=True) + 1e-6)
    along = jnp.mean(by * wide, -1, keepdims=True)
    return (by * scale - scale**3 * along * wide).astype(BF16)


def adamw(w, m, v, g):
    m = 0.9 * m + 0.1 * g
    v = 0.95 * v + 0.05 * g * g
    step = m * lax.rsqrt(v + 1e-8) + 0.1 * w
    return (w - 0.02 * step).astype(BF16), m, v


def solution(mesh):
    n = mesh.shape["dp"]

    def scatter(g):
        return lax.psum_scatter(g, "dp", scatter_dimension=0, tiled=True)

    def inner(x, dy, *arrays):
        weights, m, v = (arrays[i : i + 3] for i in (0, 3, 6))
        layers = weights[0].shape[0]
        wg, wu, wd, keep_up, keep_gate, hid0, hid1, by_gate, by_up, h1, a1 = forward(n, x[0], dy[0], *weights)
        a0, by_h = normed(x[0]), dy[0]
        g_down = mm(hid1, by_h, TN).astype(BF16)
        r0 = scatter(g_down)
        by_gate, by_up, g_down = lax.optimization_barrier((by_gate, by_up, g_down))
        g_gate = mm(a1, by_gate, TN).astype(BF16)
        r1 = scatter(g_gate)
        by_up, g_gate = lax.optimization_barrier((by_up, g_gate))
        g_up = mm(a1, by_up, TN).astype(BF16)
        r2 = scatter(g_up)
        by_gate, by_up, g_up = lax.optimization_barrier((by_gate, by_up, g_up))
        by_a = mm(by_gate, wg[1], NT).astype(BF16) + mm(by_up, wu[1], NT).astype(BF16)
        by_h = by_h + normed_back(h1, by_a)
        g_down = mm(hid0, by_h, TN).astype(BF16)
        r3 = scatter(g_down)
        by_h, g_down = lax.optimization_barrier((by_h, g_down))
        by_hidden = mm(by_h, wd[0], NT).astype(BF16).astype(F32)
        by_up, by_gate = (by_hidden * keep_up).astype(BF16), (by_hidden * keep_gate).astype(BF16)
        by_gate, by_up = lax.optimization_barrier((by_gate, by_up))
        g_gate = mm(a0, by_gate, TN).astype(BF16)
        r4 = scatter(g_gate)
        by_up, g_gate = lax.optimization_barrier((by_up, g_gate))
        r5 = scatter(mm(a0, by_up, TN).astype(BF16))
        mine = [[r4, r5, r3], [r1, r2, r0]]
        new = []
        for i in range(3):
            g = jnp.stack([mine[layer][i] for layer in range(layers)]).astype(F32)
            new.append(adamw(weights[i].astype(F32), m[i], v[i], g))
        return tuple(one[which] for which in range(3) for one in new)

    states, cut = P(("rep", "dp"), None, None), P(None, "dp", None)
    return jax.shard_map(
        inner,
        mesh=mesh,
        in_specs=(states, states) + (cut,) * 9,
        out_specs=(P("rep", "dp", None),) * 9,
        check_vma=False,
    )
```

profile of v0, /device:TPU:112, one launch (start us, length us, event | category | flops | bytes accessed | tf_op | source)
XLA Modules:
  0.0 808.3 jit_solution(4258380647441501134)
XLA Ops:
  7.2 0.1 reduce-scatter.15.cloned.1.call-start
  7.3 288.3 %forward.1 = (bf16[2,768,6144]{2,1,0:T(8,128)(2,1)}, bf16[2,768,6144]{2,1,0:T(8,128)(2,1)}, bf16[2,6144,768]{2,1,0:T(8,128)(2,1)}, f32[2048,6144]{1,0:T(8,128)},...) custom-call(bf16[2048,768]{1,0:T(8,128)(2,1)} %bitcast.54, ...), custom_call_target="tpu_custom_call" | custom-call | tf_op jit(solution)/shard_map/forward/pallas_call | solution.py:238
  295.5 26.8 %convolution_convert_fusion.6 = bf16[6144,768]{1,0:T(8,128)(2,1)} fusion(bf16[2048,6144]{1,0:T(8,128)(2,1)} %get-tuple-element.31, bf16[1,2048,768]{2,1,0:T(8,128)(2,1)} %param.12), kind=kOutput, calls=%fused_computation.10 | convolution fusion | flops 19332071424 | bytes 37748736 | tf_op jit(solution)/shard_map/dot_general | solution.py:17
  322.4 25.3 %convolution_convert_fusion.4 = bf16[768,6144]{1,0:T(8,128)(2,1)} fusion(bf16[2048,768]{1,0:T(8,128)(2,1)S(1)} %copy-done.6, bf16[2048,6144]{1,0:T(8,128)(2,1)} %get-tuple-element.36), kind=kOutput, calls=%fused_computation.8 | convolution fusion | flops 19332071424 | bytes 37748736 | tf_op jit(solution)/shard_map/dot_general | solution.py:17
  347.7 25.8 %convolution_convert_fusion.3 = bf16[768,6144]{1,0:T(8,128)(2,1)} fusion(bf16[2048,768]{1,0:T(8,128)(2,1)S(1)} %copy-done.6, bf16[2048,6144]{1,0:T(8,128)(2,1)} %get-tuple-element.38), kind=kOutput, calls=%fused_computation.7 | convolution fusion | flops 19332071424 | bytes 37748736 | tf_op jit(solution)/shard_map/dot_general | solution.py:17
  373.4 26.8 %fusion.31 = bf16[2048,768]{1,0:T(8,128)(2,1)} fusion(bf16[2048,6144]{1,0:T(8,128)(2,1)} %get-tuple-element.36, bf16[2,768,6144]{2,1,0:T(8,128)(2,1)} %get-tuple-element.37), kind=kOutput, calls=%fused_computation.58 | convolution fusion | flops 19328925696 | bytes 37748736 | tf_op jit(solution)/shard_map/dot_general | solution.py:17
  400.3 27.7 %fusion.14 = (f32[2048]{0:T(1024)S(1)}, f32[2048]{0:T(1024)S(1)}, bf16[2048,768]{1,0:T(8,128)(2,1)}) fusion(bf16[2048,768]{1,0:T(8,128)(2,1)S(1)} %copy-done.5, bf16[2048,768]{1,0:T(8,128)(2,1)} %fusion.31, bf16[2048,6144]{1,0:T(8,128)(2,1)} %get-tuple-element.38, bf16[2,768,6144]{2,1,0:T(8,128)(2,1)} %get-tuple-element.39), kind=kOutput, calls=%fused_computation.32 | convolution fusion | flops 19339931648 | bytes 44056576 | tf_op jit(solution)/shard_map/dot_general | solution.py:17
  427.9 3.2 fusion.37
  431.1 1.7 copy-done.2
  432.8 26.1 %convolution_convert_fusion.5 = bf16[6144,768]{1,0:T(8,128)(2,1)} fusion(bf16[2048,6144]{1,0:T(8,128)(2,1)} %get-tuple-element.41, bf16[2048,768]{1,0:T(8,128)(2,1)S(1)} %fusion.37), kind=kOutput, calls=%fused_computation.9 | convolution fusion | flops 19332071424 | bytes 37748736 | tf_op jit(solution)/shard_map/dot_general | solution.py:17
  458.9 0.1 reduce-scatter.15.cloned.1.call-update
  459.0 0.1 reduce-scatter.17.cloned.1.call-start
  459.1 0.7 reduce-scatter.17.cloned.1.call-update
  459.8 0.1 reduce-scatter.11.cloned.1.call-start
  459.9 58.6 %fusion.1 = (bf16[2048,6144]{1,0:T(8,128)(2,1)}, bf16[2048,6144]{1,0:T(8,128)(2,1)}) fusion(f32[2048,6144]{1,0:T(8,128)} %get-tuple-element.45, f32[2048,6144]{1,0:T(8,128)} %get-tuple-element.44, bf16[2048,768]{1,0:T(8,128)(2,1)} %copy-done.2, bf16[2,6144,768]{2,1,0:T(8,128)(2,1)} %get-tuple-element.43), kind=kOutput, calls=%fused_computation.3 | convolution fusion | flops 19402850304 | bytes 163577856 | tf_op jit(solution)/shard_map/dot_general | solution.py:17
  518.5 0.7 fusion.10
  519.2 26.7 %convolution_convert_fusion.2 = bf16[768,6144]{1,0:T(8,128)(2,1)} fusion(bf16[2048,6144]{1,0:T(8,128)(2,1)} %get-tuple-element.46, f32[2048]{0:T(1024)S(1)} %add_rsqrt_fusion.1, bf16[1,2048,768]{2,1,0:T(8,128)(2,1)S(1)} %copy-done), kind=kOutput, calls=%fused_computation.6 | convolution fusion | flops 19336790016 | bytes 37756928 | tf_op jit(solution)/shard_map/dot_general | solution.py:17
  546.0 26.2 %convolution_convert_fusion.1 = bf16[768,6144]{1,0:T(8,128)(2,1)} fusion(bf16[2048,6144]{1,0:T(8,128)(2,1)} %get-tuple-element.48, f32[2048]{0:T(1024)S(1)} %add_rsqrt_fusion.1, bf16[1,2048,768]{2,1,0:T(8,128)(2,1)S(1)} %copy-done), kind=kOutput, calls=%fused_computation.5 | convolution fusion | flops 19336790016 | bytes 37756928 | tf_op jit(solution)/shard_map/dot_general | solution.py:17
  572.3 0.1 reduce-scatter.13.cloned.1.call-start
  572.3 0.6 reduce-scatter.13.cloned.1.call-update
  572.9 0.1 reduce-scatter.7.cloned.1.call-start
  573.0 0.6 reduce-scatter.7.cloned.1.call-update
  573.6 0.1 reduce-scatter.9.cloned.1.call-start
  573.6 0.6 reduce-scatter.9.cloned.1.call-update
  574.2 1.0 copy-done.3
  575.2 9.8 %fusion.26 = (bf16[2,768,768]{2,1,0:T(8,128)(2,1)}, f32[2,768,768]{2,1,0:T(8,128)}, f32[2,768,768]{2,1,0:T(8,128)}) fusion(bf16[2,768,768]{2,1,0:T(8,128)(2,1)S(1)} %copy-done.3, bf16[1,768,768]{2,1,0:T(8,128)(2,1)} %bitcast.57, bf16[1,768,768]{2,1,0:T(8,128)(2,1)} %bitcast.56, f32[2,768,768]{2,1,0:T(8,128)} %param.21, f32[2,768,768]{2,1,0:T(8,128)} %param.18), kind=kLoop, calls=%fused_computation.53 | loop fusion | flops 22413312 | bytes 25952256 | tf_op jit(solution)/shard_map/convert_element_type | solution.py:270
  585.0 42.2 %reduce-scatter.11.cloned.1.call-done = bf16[96,6144]{1,0:T(8,128)(2,1)} async-done(((bf16[768,6144]{1,0:T(8,128)(2,1)}), bf16[96,6144]{1,0:T(8,128)(2,1)}) %reduce-scatter.11.cloned.1.call-update) | async-done | bytes 1179664 | tf_op jit(solution)/shard_map/reduce_scatter | solution.py:277
  627.2 55.1 %reduce-scatter.13.cloned.1.call-done = bf16[96,6144]{1,0:T(8,128)(2,1)} async-done(((bf16[768,6144]{1,0:T(8,128)(2,1)}), bf16[96,6144]{1,0:T(8,128)(2,1)}) %reduce-scatter.13.cloned.1.call-update) | async-done | bytes 1179664 | tf_op jit(solution)/shard_map/reduce_scatter | solution.py:277
  682.4 9.3 %fusion.22 = (bf16[2,96,6144]{2,1,0:T(8,128)(2,1)}, f32[2,96,6144]{2,1,0:T(8,128)}, f32[2,96,6144]{2,1,0:T(8,128)}) fusion(bf16[2,96,6144]{2,1,0:T(8,128)(2,1)} %su.1, bf16[1,96,6144]{2,1,0:T(8,128)(2,1)} %bitcast.60, bf16[1,96,6144]{2,1,0:T(8,128)(2,1)} %bitcast.58, f32[2,96,6144]{2,1,0:T(8,128)} %param.20, f32[2,96,6144]{2,1,0:T(8,128)} %param.17), kind=kLoop, calls=%fused_computation.49 | loop fusion | flops 22413312 | bytes 25952256 | tf_op jit(solution)/shard_map/convert_element_type | solution.py:270
  691.6 45.9 %reduce-scatter.7.cloned.1.call-done = bf16[96,6144]{1,0:T(8,128)(2,1)} async-done(((bf16[768,6144]{1,0:T(8,128)(2,1)}), bf16[96,6144]{1,0:T(8,128)(2,1)}) %reduce-scatter.7.cloned.1.call-update) | async-done | bytes 1179664 | tf_op jit(solution)/shard_map/reduce_scatter | solution.py:277
  737.5 55.1 %reduce-scatter.9.cloned.1.call-done = bf16[96,6144]{1,0:T(8,128)(2,1)} async-done(((bf16[768,6144]{1,0:T(8,128)(2,1)}), bf16[96,6144]{1,0:T(8,128)(2,1)}) %reduce-scatter.9.cloned.1.call-update) | async-done | bytes 1179664 | tf_op jit(solution)/shard_map/reduce_scatter | solution.py:277
  792.7 8.4 %fusion.18 = (bf16[2,96,6144]{2,1,0:T(8,128)(2,1)}, f32[2,96,6144]{2,1,0:T(8,128)}, f32[2,96,6144]{2,1,0:T(8,128)}) fusion(bf16[2,96,6144]{2,1,0:T(8,128)(2,1)S(1)} %copy-done.4, bf16[1,96,6144]{2,1,0:T(8,128)(2,1)} %bitcast.61, bf16[1,96,6144]{2,1,0:T(8,128)(2,1)} %bitcast.59, f32[2,96,6144]{2,1,0:T(8,128)} %param.19, f32[2,96,6144]{2,1,0:T(8,128)} %param.16), kind=kLoop, calls=%fused_computation.45 | loop fusion | flops 22413312 | bytes 25952256 | tf_op jit(solution)/shard_map/convert_element_type | solution.py:270
  (17 shorter events, 0.1 us)
Async XLA Ops:
  7.2 567.0 %reduce-scatter.15.cloned.1.call-start = ((), (), s32[]{:S(2)}) async-start(), calls=%async_computation.10 | async-start | bytes 10616832 | tf_op jit(solution)/shard_map/reduce_scatter | solution.py:277
  295.5 26.9 %copy-start.6 = (bf16[2048,768]{1,0:T(8,128)(2,1)S(1)}, bf16[2048,768]{1,0:T(8,128)(2,1)}, u32[]{:S(2)}) copy-start(bf16[2048,768]{1,0:T(8,128)(2,1)} %get-tuple-element.34) | copy-start | bytes 9437188
  373.4 26.8 %copy-start.5 = (bf16[2048,768]{1,0:T(8,128)(2,1)S(1)}, bf16[2048,768]{1,0:T(8,128)(2,1)}, u32[]{:S(2)}) copy-start(bf16[2048,768]{1,0:T(8,128)(2,1)} %get-tuple-element.40) | copy-start | bytes 9437188
  400.3 27.7 %copy-start.1 = (bf16[1,2048,768]{2,1,0:T(8,128)(2,1)S(1)}, bf16[1,2048,768]{2,1,0:T(8,128)(2,1)}, u32[]{:S(2)}) copy-start(bf16[1,2048,768]{2,1,0:T(8,128)(2,1)} %param.12) | copy-start | bytes 9437188
  431.1 1.7 copy-start.2
  459.0 115.2 %reduce-scatter.17.cloned.1.call-start = ((), (), s32[]{:S(2)}) async-start(), calls=%async_computation.11 | async-start | bytes 10616832 | tf_op jit(solution)/shard_map/reduce_scatter | solution.py:277
  459.8 167.4 %reduce-scatter.11.cloned.1.call-start = ((), (), s32[]{:S(2)}) async-start(), calls=%async_computation.8 | async-start | bytes 10616832 | tf_op jit(solution)/shard_map/reduce_scatter | solution.py:277
  459.9 58.6 %copy-start = (bf16[1,2048,768]{2,1,0:T(8,128)(2,1)S(1)}, bf16[1,2048,768]{2,1,0:T(8,128)(2,1)}, u32[]{:S(2)}) copy-start(bf16[1,2048,768]{2,1,0:T(8,128)(2,1)} %param.11) | copy-start | bytes 9437188
  572.3 110.1 %reduce-scatter.13.cloned.1.call-start = ((), (), s32[]{:S(2)}) async-start(), calls=%async_computation.9 | async-start | bytes 10616832 | tf_op jit(solution)/shard_map/reduce_scatter | solution.py:277
  572.9 164.6 %reduce-scatter.7.cloned.1.call-start = ((), (), s32[]{:S(2)}) async-start(), calls=%async_computation.6 | async-start | bytes 10616832 | tf_op jit(solution)/shard_map/reduce_scatter | solution.py:277
  573.5 1.7 copy-start.3
  573.6 219.1 %reduce-scatter.9.cloned.1.call-start = ((), (), s32[]{:S(2)}) async-start(), calls=%async_computation.7 | async-start | bytes 10616832 | tf_op jit(solution)/shard_map/reduce_scatter | solution.py:277
  682.4 110.3 %copy-start.4 = (bf16[2,96,6144]{2,1,0:T(8,128)(2,1)S(1)}, bf16[2,96,6144]{2,1,0:T(8,128)(2,1)}, u32[]{:S(2)}) copy-start(bf16[2,96,6144]{2,1,0:T(8,128)(2,1)} %sg.1) | copy-start | bytes 7077892
Sparse Core Ops, SparseCore 0:
  459.1 54.7 reduce-scatter.14
  516.2 52.9 reduce-scatter.16
  572.4 54.7 reduce-scatter.10
  629.4 52.9 reduce-scatter.12
  684.5 52.9 reduce-scatter.6
  739.7 52.9 reduce-scatter.8
where the time goes:
time: 816 us; the launch traced here: 808 us
  Pallas kernels  288 us (35%)
  matrix products  270 us (33%)
  waiting for transfers between devices  201 us (25%)
  other arithmetic  31.3 us (4%)
  between operations  14.7 us (2%)
    pallas_call x1, Pallas kernels, forward(): pl.pallas_call(functools.partial(forward_kernel, n), out_shape=(s((layers...  288 us
    dot_general x9, matrix products, mm(): return lax.dot_general(a, w, (dims, ((), ())), preferred_element_type=F32)  270 us
    reduce_scatter x6, waiting for transfers between devices, scatter(): return lax.psum_scatter(g, 'dp', scatter_dimension=0, tiled=True)  198 us
    convert_element_type x3, other arithmetic, adamw(): return ((w - 0.02 * step).astype(BF16), m, v)  27.4 us
  transfers between devices with their start and end apart: 6, of which 4 were waited for; matrix products, arithmetic and copies ran while one was open for 16% of the time, Pallas kernels for 0%

commit v1 on v0

--- a/solution.py
+++ b/solution.py
@@ -256,6 +256,165 @@
     )(x, dy, sg, su, sd)
 
 
+def tail_kernel(n, by_ref, at_ref, wd, keep_up, keep_gate, out, bg, bu, term, there, own, hold, first, second, far_a, far_b, low, high, send, recv):
+    me = lax.axis_index("dp")
+    chip, core = me // 2, lax.rem(me, 2)
+    ring = n // 2
+    at = lambda c, k: 2 * lax.rem(c, ring) + k
+    right, left, partner = at(chip + 1, core), at(chip + ring - 1, core), at(chip, 1 - core)
+
+    barrier = pltpu.get_barrier_semaphore()
+    for other in (left, right, partner):
+        pl.semaphore_signal(barrier, inc=1, device_id={"dp": other}, device_id_type=MESH)
+    pl.semaphore_wait(barrier, 3)
+
+    tokens, d = by_ref.shape
+    slices, bn = there.shape[0], there.shape[-1]
+    slots = hold.shape[0]
+
+    def move(u, kind):
+        slot = lax.rem(u, slots)
+        source, target, to = [
+            (term.at[lax.rem(u, 2), :, :, 1 - core], there.at[u], partner),
+            (first.at[slot, 0], far_a.at[u], right),
+            (first.at[slot, 1], far_b.at[u], left),
+            (first.at[slot, 2], low.at[u, 1], right),
+            (first.at[slot, 3], high.at[u, 0], left),
+            (second.at[slot, 0], low.at[u, 0], right),
+            (second.at[slot, 1], high.at[u, 1], left),
+        ][kind]
+        return pltpu.make_async_remote_copy(
+            src_ref=source, dst_ref=target, send_sem=send.at[u, kind], recv_sem=recv.at[u, kind], device_id={"dp": to}, device_id_type=MESH
+        )
+
+    def pair_sum(u):
+        slot, turn = lax.rem(u, slots), lax.rem(u, 2)
+        move(u, 0).wait_recv()
+
+        @pl.when(u >= slots)
+        def _():
+            for kind in (1, 2, 3, 4):
+                move(u - slots, kind).wait_send()
+
+        def both(away, which):
+            c = lax.rem(chip + away, ring)
+            return term[turn, which, c, core].astype(F32) + there[u, which, c].astype(F32)
+
+        for i, (away, which) in enumerate(((2, 0), (2, 1), (1, 1), (ring - 1, 0))):
+            first[slot, i] = both(away, which).astype(BF16)
+        for kind in (1, 2, 3, 4):
+            move(u, kind).start()
+        hold[slot, 0] = both(1, 0)
+        hold[slot, 1] = both(ring - 1, 1)
+        for which in range(2):
+            own[u, which] = both(0, which)
+
+    def add_far(u):
+        slot = lax.rem(u, slots)
+
+        @pl.when(u >= slots)
+        def _():
+            for kind in (5, 6):
+                move(u - slots, kind).wait_send()
+
+        for i, far in enumerate((far_a, far_b)):
+            move(u, 1 + i).wait_recv()
+            second[slot, i] = (hold[slot, i] + far[u].astype(F32)).astype(BF16)
+            move(u, 5 + i).start()
+
+    def finish(u):
+        for kind in (3, 4, 5, 6):
+            move(u, kind).wait_recv()
+        columns = pl.ds(pl.multiple_of(u * bn, bn), bn)
+        for which in range(2):
+            total = own[u, which] + low[u, which].astype(F32) + high[u, which].astype(F32)
+            out[which, :, columns] = total.astype(BF16)
+
+    bm, sub = tokens // 2, 256
+
+    def body(d_ref, ku_ref, kg_ref):
+        j, i = pl.program_id(0), pl.program_id(1)
+
+        @pl.when((i == 0) & (j >= 3))
+        def _():
+            finish(j - 3)
+
+        @pl.when((i == 0) & (j >= 2))
+        def _():
+            add_far(j - 2)
+
+        for r in range(0, bm, sub):
+            here, whole = pl.ds(r, sub), pl.ds(pl.multiple_of(i * bm + r, sub), sub)
+            by = mm(by_ref[whole, :], d_ref[...], NT).astype(BF16).astype(F32)
+            bu[whole, :] = (by * ku_ref[here, :]).astype(BF16)
+            bg[whole, :] = (by * kg_ref[here, :]).astype(BF16)
+
+        @pl.when((i == 0) & (j >= 1))
+        def _():
+            pair_sum(j - 1)
+
+        @pl.when(i == 1)
+        def _():
+            @pl.when(j >= 2)
+            def _():
+                move(j - 2, 0).wait_send()
+
+            for which, by in enumerate((bg, bu)):
+                g = jnp.dot(at_ref[...], by[...], preferred_element_type=F32).astype(BF16)
+                term[lax.rem(j, 2), which] = g.reshape(term.shape[2:])
+            move(j, 0).start()
+
+    tile = pl.BlockSpec((bm, bn), lambda j, i: (i, j))
+    pltpu.emit_pipeline(
+        body, grid=(slices, 2), in_specs=[pl.BlockSpec((bn, d), lambda j, i: (j, 0)), tile, tile], out_specs=[]
+    )(wd.at[0], keep_up, keep_gate)
+
+    finish(slices - 3)
+    add_far(slices - 2)
+    pair_sum(slices - 1)
+    finish(slices - 2)
+    add_far(slices - 1)
+    finish(slices - 1)
+    for u in range(slices - 2, slices):
+        move(u, 0).wait_send()
+    for u in range(slices - slots, slices):
+        for kind in range(1, 7):
+            move(u, kind).wait_send()
+
+
+def tail(n, by_h, a, wd, keep_up, keep_gate):
+    tokens, d = by_h.shape
+    ff = keep_up.shape[1]
+    depth, bn = d // n, 512
+    slices, slots, ring = ff // bn, 4, n // 2
+    vmem, hbm = pl.BlockSpec(memory_space=pltpu.VMEM), pl.BlockSpec(memory_space=pl.ANY)
+    block = (depth, bn)
+    return pl.pallas_call(
+        functools.partial(tail_kernel, n),
+        out_shape=jax.ShapeDtypeStruct((2, depth, ff), BF16),
+        in_specs=[vmem, vmem, hbm, hbm, hbm],
+        out_specs=vmem,
+        scratch_shapes=[
+            pltpu.VMEM((tokens, bn), BF16),
+            pltpu.VMEM((tokens, bn), BF16),
+            pltpu.VMEM((2, 2, ring, 2) + block, BF16),
+            pltpu.VMEM((slices, 2, ring) + block, BF16),
+            pltpu.VMEM((slices, 2) + block, F32),
+            pltpu.VMEM((slots, 2) + block, F32),
+            pltpu.VMEM((slots, 4) + block, BF16),
+            pltpu.VMEM((slots, 2) + block, BF16),
+            pltpu.VMEM((slices,) + block, BF16),
+            pltpu.VMEM((slices,) + block, BF16),
+            pltpu.VMEM((slices, 2) + block, BF16),
+            pltpu.VMEM((slices, 2) + block, BF16),
+            pltpu.SemaphoreType.DMA((slices, 7)),
+            pltpu.SemaphoreType.DMA((slices, 7)),
+        ],
+        compiler_params=pltpu.CompilerParams(collective_id=1, has_side_effects=True, vmem_limit_bytes=63 * 1024 * 1024),
+        name="tail",
+    )(by_h, a.T, wd, keep_up, keep_gate)
+
+
 def normed_back(h, by_a):
     wide, by = h.astype(F32), by_a.astype(F32)
     scale = lax.rsqrt(jnp.mean(wide**2, -1, keepdims=True) + 1e-6)
@@ -295,13 +454,7 @@
         g_down = mm(hid0, by_h, TN).astype(BF16)
         r3 = scatter(g_down)
         by_h, g_down = lax.optimization_barrier((by_h, g_down))
-        by_hidden = mm(by_h, wd[0], NT).astype(BF16).astype(F32)
-        by_up, by_gate = (by_hidden * keep_up).astype(BF16), (by_hidden * keep_gate).astype(BF16)
-        by_gate, by_up = lax.optimization_barrier((by_gate, by_up))
-        g_gate = mm(a0, by_gate, TN).astype(BF16)
-        r4 = scatter(g_gate)
-        by_up, g_gate = lax.optimization_barrier((by_up, g_gate))
-        r5 = scatter(mm(a0, by_up, TN).astype(BF16))
+        r4, r5 = tail(n, by_h, a0, wd, keep_up, keep_gate)
         mine = [[r4, r5, r3], [r1, r2, r0]]
         new = []
         for i in range(3):

time: 816 us -> 758 us (0.929)
  Pallas kernels: 288 us -> 408 us
  matrix products: 270 us -> 159 us
  waiting for transfers between devices: 201 us -> 129 us
    pallas_call x0 -> x1, Pallas kernels: none -> 130 us  [tail(): pl.pallas_call(functools.partial(tail_kernel, n), out_shape=jax.ShapeDtyp...]
    dot_general x9 -> x6, matrix products: 270 us -> 159 us  [mm(): return lax.dot_general(a, w, (dims, ((), ())), preferred_element_type=F32)]
    reduce_scatter x6 -> x4, waiting for transfers between devices: 198 us -> 127 us  [scatter(): return lax.psum_scatter(g, 'dp', scatter_dimension=0, tiled=True)]
    pallas_call x1, Pallas kernels: 288 us -> 278 us  [forward(): pl.pallas_call(functools.partial(forward_kernel, n), out_shape=(s((layers...]
  transfers between devices with their start and end apart: 6 -> 4, of which waited for: 4 -> 3; matrix products, arithmetic and copies ran while one was open for 16% -> 4% of each run, Pallas kernels for 0% -> 17%
where the time goes in v1:
time: 758 us; the launch traced here: 750 us
  Pallas kernels  408 us (54%)
  matrix products  159 us (21%)
  waiting for transfers between devices  129 us (17%)
  other arithmetic  32.4 us (4%)
  between operations  14.3 us (2%)
  local copies, waits for them, and re-layouts  8.13 us (1%)
    pallas_call x1, Pallas kernels, forward(): pl.pallas_call(functools.partial(forward_kernel, n), out_shape=(s((layers...  278 us
    dot_general x6, matrix products, mm(): return lax.dot_general(a, w, (dims, ((), ())), preferred_element_type=F32)  159 us
    pallas_call x1, Pallas kernels, tail(): pl.pallas_call(functools.partial(tail_kernel, n), out_shape=jax.ShapeDtyp...  130 us
    reduce_scatter x4, waiting for transfers between devices, scatter(): return lax.psum_scatter(g, 'dp', scatter_dimension=0, tiled=True)  127 us
    convert_element_type x3, other arithmetic, adamw(): return ((w - 0.02 * step).astype(BF16), m, v)  26.1 us
  transfers between devices with their start and end apart: 4, of which 3 were waited for; matrix products, arithmetic and copies ran while one was open for 4% of the time, Pallas kernels for 17%

profile of v1, /device:TPU:112, one launch (start us, length us, event | category | flops | bytes accessed | tf_op | source)
XLA Modules:
  0.0 750.3 jit_solution(2279661341032197897)
XLA Ops:
  7.2 0.1 reduce-scatter.9.cloned.1.call-start
  7.3 278.3 %forward.1 = (bf16[2,768,6144]{2,1,0:T(8,128)(2,1)}, bf16[2,768,6144]{2,1,0:T(8,128)(2,1)}, bf16[2,6144,768]{2,1,0:T(8,128)(2,1)}, f32[2048,6144]{1,0:T(8,128)},...) custom-call(bf16[2048,768]{1,0:T(8,128)(2,1)} %bitcast.37, ...), custom_call_target="tpu_custom_call" | custom-call | tf_op jit(solution)/shard_map/forward/pallas_call | solution.py:238
  285.6 0.0 copy-start.5
  285.6 26.9 %convolution_convert_fusion.3 = bf16[6144,768]{1,0:T(8,128)(2,1)} fusion(bf16[2048,6144]{1,0:T(8,128)(2,1)} %get-tuple-element.28, bf16[1,2048,768]{2,1,0:T(8,128)(2,1)} %param.12), kind=kOutput, calls=%fused_computation.3 | convolution fusion | flops 19332071424 | bytes 37748736 | tf_op jit(solution)/shard_map/dot_general | solution.py:17
  312.4 0.0 copy-done.5
  312.4 25.4 %convolution_convert_fusion.1 = bf16[768,6144]{1,0:T(8,128)(2,1)} fusion(bf16[2048,768]{1,0:T(8,128)(2,1)S(1)} %copy-done.5, bf16[2048,6144]{1,0:T(8,128)(2,1)} %get-tuple-element.33), kind=kOutput, calls=%fused_computation.1 | convolution fusion | flops 19332071424 | bytes 37748736 | tf_op jit(solution)/shard_map/dot_general | solution.py:17
  337.9 25.6 %convolution_convert_fusion = bf16[768,6144]{1,0:T(8,128)(2,1)} fusion(bf16[2048,768]{1,0:T(8,128)(2,1)S(1)} %copy-done.5, bf16[2048,6144]{1,0:T(8,128)(2,1)} %get-tuple-element.35), kind=kOutput, calls=%fused_computation | convolution fusion | flops 19332071424 | bytes 37748736 | tf_op jit(solution)/shard_map/dot_general | solution.py:17
  363.5 26.8 %fusion.27 = bf16[2048,768]{1,0:T(8,128)(2,1)} fusion(bf16[2048,6144]{1,0:T(8,128)(2,1)} %get-tuple-element.33, bf16[2,768,6144]{2,1,0:T(8,128)(2,1)} %get-tuple-element.34), kind=kOutput, calls=%fused_computation.49 | convolution fusion | flops 19328925696 | bytes 37748736 | tf_op jit(solution)/shard_map/dot_general | solution.py:17
  390.3 27.7 %fusion.10 = (f32[2048]{0:T(1024)S(1)}, f32[2048]{0:T(1024)S(1)}, bf16[2048,768]{1,0:T(8,128)(2,1)}) fusion(bf16[2048,768]{1,0:T(8,128)(2,1)S(1)} %copy-done.4, bf16[2048,768]{1,0:T(8,128)(2,1)} %fusion.27, bf16[2048,6144]{1,0:T(8,128)(2,1)} %get-tuple-element.35, bf16[2,768,6144]{2,1,0:T(8,128)(2,1)} %get-tuple-element.36), kind=kOutput, calls=%fused_computation.23 | convolution fusion | flops 19339931648 | bytes 44056576 | tf_op jit(solution)/shard_map/dot_general | solution.py:17
  418.1 3.2 fusion.34.by_ref
  421.3 0.0 copy-start.1
  421.3 1.7 copy-done.1
  422.9 26.1 %convolution_convert_fusion.2 = bf16[6144,768]{1,0:T(8,128)(2,1)} fusion(bf16[2048,6144]{1,0:T(8,128)(2,1)} %get-tuple-element.38, bf16[2048,768]{1,0:T(8,128)(2,1)S(1)} %fusion.34.by_ref), kind=kOutput, calls=%fused_computation.2 | convolution fusion | flops 19332071424 | bytes 37748736 | tf_op jit(solution)/shard_map/dot_general | solution.py:17
  449.0 0.1 reduce-scatter.9.cloned.1.call-update
  449.1 0.1 reduce-scatter.11.cloned.1.call-start
  449.1 0.7 reduce-scatter.11.cloned.1.call-update
  449.9 0.1 reduce-scatter.7.cloned.1.call-start
  450.0 0.7 reduce-scatter.7.cloned.1.call-update
  450.7 0.1 reduce-scatter.5.cloned.1.call-start
  450.7 0.6 reduce-scatter.5.cloned.1.call-update
  451.3 3.4 copy.20
  454.8 0.7 fusion.8
  455.4 2.4 fusion.33.at_ref
  457.9 129.7 %tail.1 = bf16[2,96,6144]{2,1,0:T(8,128)(2,1)} custom-call(bf16[2048,768]{1,0:T(8,128)(2,1)} %copy-done.1, bf16[768,2048]{1,0:T(8,128)(2,1)} %fusion.33.at_ref, bf16[2,6144,768]{2,1,0:T(8,128)(2,1)} %get-tuple-element.40.wd, f32[2048,6144]{1,0:T(8,128)} %get-tuple-element.41.keep_up, f32[2048,6144]{1,0:T(8,128)} %get-tuple-element.42.keep_gate), custom_call_target="tpu_custom_call" | custom-call | tf_op jit(solution)/shard_map/tail/pallas_call | solution.py:392
  587.6 0.0 copy-start.2
  587.6 3.0 fusion.46
  590.6 33.5 %reduce-scatter.11.cloned.1.call-done = bf16[768,768]{1,0:T(8,128)(2,1)} async-done(((bf16[6144,768]{1,0:T(8,128)(2,1)}), bf16[768,768]{1,0:T(8,128)(2,1)}) %reduce-scatter.11.cloned.1.call-update) | async-done | bytes 1179664 | tf_op jit(solution)/shard_map/reduce_scatter | solution.py:436
  624.1 8.6 %fusion.22 = (bf16[2,768,768]{2,1,0:T(8,128)(2,1)}, f32[2,768,768]{2,1,0:T(8,128)}, f32[2,768,768]{2,1,0:T(8,128)}) fusion(bf16[2,768,768]{2,1,0:T(8,128)(2,1)S(1)} %copy-done.2, bf16[1,768,768]{2,1,0:T(8,128)(2,1)} %bitcast.42, bf16[1,768,768]{2,1,0:T(8,128)(2,1)} %bitcast.39, f32[2,768,768]{2,1,0:T(8,128)} %param.21, f32[2,768,768]{2,1,0:T(8,128)} %param.18), kind=kLoop, calls=%fused_computation.44 | loop fusion | flops 22413312 | bytes 25952256 | tf_op jit(solution)/shard_map/convert_element_type | solution.py:429
  632.7 47.2 %reduce-scatter.7.cloned.1.call-done = bf16[96,6144]{1,0:T(8,128)(2,1)} async-done(((bf16[768,6144]{1,0:T(8,128)(2,1)}), bf16[96,6144]{1,0:T(8,128)(2,1)}) %reduce-scatter.7.cloned.1.call-update) | async-done | bytes 1179664 | tf_op jit(solution)/shard_map/reduce_scatter | solution.py:436
  680.0 9.3 %fusion.18 = (bf16[2,96,6144]{2,1,0:T(8,128)(2,1)}, f32[2,96,6144]{2,1,0:T(8,128)}, f32[2,96,6144]{2,1,0:T(8,128)}) fusion(bf16[2,96,6144]{2,1,0:T(8,128)(2,1)} %su.1, bf16[1,96,6144]{2,1,0:T(8,128)(2,1)} %bitcast.41, bf16[1,96,6144]{2,1,0:T(8,128)(2,1)} %get-tuple-element.54, f32[2,96,6144]{2,1,0:T(8,128)} %param.20, f32[2,96,6144]{2,1,0:T(8,128)} %param.17), kind=kLoop, calls=%fused_computation.40 | loop fusion | flops 22413312 | bytes 25952256 | tf_op jit(solution)/shard_map/convert_element_type | solution.py:429
  689.2 45.9 %reduce-scatter.5.cloned.1.call-done = bf16[96,6144]{1,0:T(8,128)(2,1)} async-done(((bf16[768,6144]{1,0:T(8,128)(2,1)}), bf16[96,6144]{1,0:T(8,128)(2,1)}) %reduce-scatter.5.cloned.1.call-update) | async-done | bytes 1179664 | tf_op jit(solution)/shard_map/reduce_scatter | solution.py:436
  735.1 8.2 %fusion.14 = (bf16[2,96,6144]{2,1,0:T(8,128)(2,1)}, f32[2,96,6144]{2,1,0:T(8,128)}, f32[2,96,6144]{2,1,0:T(8,128)}) fusion(bf16[2,96,6144]{2,1,0:T(8,128)(2,1)S(1)} %copy-done.3, bf16[1,96,6144]{2,1,0:T(8,128)(2,1)} %bitcast.40, bf16[1,96,6144]{2,1,0:T(8,128)(2,1)S(1)} %get-tuple-element.55, f32[2,96,6144]{2,1,0:T(8,128)} %param.19, f32[2,96,6144]{2,1,0:T(8,128)} %param.16), kind=kLoop, calls=%fused_computation.36 | loop fusion | flops 22413312 | bytes 25952256 | tf_op jit(solution)/shard_map/convert_element_type | solution.py:429
  (10 shorter events, 0.0 us)
Async XLA Ops:
  7.2 583.4 %reduce-scatter.9.cloned.1.call-start = ((), (), s32[]{:S(2)}) async-start(), calls=%async_computation.6 | async-start | bytes 10616832 | tf_op jit(solution)/shard_map/reduce_scatter | solution.py:436
  285.6 26.9 %copy-start.5 = (bf16[2048,768]{1,0:T(8,128)(2,1)S(1)}, bf16[2048,768]{1,0:T(8,128)(2,1)}, u32[]{:S(2)}) copy-start(bf16[2048,768]{1,0:T(8,128)(2,1)} %get-tuple-element.31) | copy-start | bytes 9437188
  363.5 26.8 %copy-start.4 = (bf16[2048,768]{1,0:T(8,128)(2,1)S(1)}, bf16[2048,768]{1,0:T(8,128)(2,1)}, u32[]{:S(2)}) copy-start(bf16[2048,768]{1,0:T(8,128)(2,1)} %get-tuple-element.37) | copy-start | bytes 9437188
  390.3 27.7 %copy-start = (bf16[1,2048,768]{2,1,0:T(8,128)(2,1)S(1)}, bf16[1,2048,768]{2,1,0:T(8,128)(2,1)}, u32[]{:S(2)}) copy-start(bf16[1,2048,768]{2,1,0:T(8,128)(2,1)} %param.12) | copy-start | bytes 9437188
  421.3 1.7 copy-start.1
  449.1 175.0 %reduce-scatter.11.cloned.1.call-start = ((), (), s32[]{:S(2)}) async-start(), calls=%async_computation.7 | async-start | bytes 10616832 | tf_op jit(solution)/shard_map/reduce_scatter | solution.py:436
  449.9 230.1 %reduce-scatter.7.cloned.1.call-start = ((), (), s32[]{:S(2)}) async-start(), calls=%async_computation.5 | async-start | bytes 10616832 | tf_op jit(solution)/shard_map/reduce_scatter | solution.py:436
  450.7 284.4 %reduce-scatter.5.cloned.1.call-start = ((), (), s32[]{:S(2)}) async-start(), calls=%async_computation.4 | async-start | bytes 10616832 | tf_op jit(solution)/shard_map/reduce_scatter | solution.py:436
  587.6 36.5 %copy-start.2 = (bf16[2,768,768]{2,1,0:T(8,128)(2,1)S(1)}, bf16[2,768,768]{2,1,0:T(8,128)(2,1)}, u32[]{:S(2)}) copy-start(bf16[2,768,768]{2,1,0:T(8,128)(2,1)} %sd.1) | copy-start | bytes 7077892
  680.0 55.2 %copy-start.3 = (bf16[2,96,6144]{2,1,0:T(8,128)(2,1)S(1)}, bf16[2,96,6144]{2,1,0:T(8,128)(2,1)}, u32[]{:S(2)}) copy-start(bf16[2,96,6144]{2,1,0:T(8,128)(2,1)} %sg.1) | copy-start | bytes 7077892
Sparse Core Ops, SparseCore 0:
  449.2 108.1 reduce-scatter.8
  559.7 64.3 reduce-scatter.10
  626.4 53.5 reduce-scatter.6
  682.1 52.9 reduce-scatter.4

commit v2 on v1

--- a/solution.py
+++ b/solution.py
@@ -23,7 +23,14 @@
     return (wide * scale).astype(BF16)
 
 
-def forward_kernel(n, x_ref, dy_ref, sg, su, sd, wg, wu, wd, keep_up, keep_gate, hid0, hid1, by_gate, by_up, h1, a1, a0, wd_v, send, recv, local, load):
+def normed_back(h, by_a):
+    wide, by = h.astype(F32), by_a.astype(F32)
+    scale = lax.rsqrt(jnp.mean(wide**2, -1, keepdims=True) + 1e-6)
+    along = jnp.mean(by * wide, -1, keepdims=True)
+    return (by * scale - scale**3 * along * wide).astype(BF16)
+
+
+def forward_kernel(n, x_ref, dy, sg, su, sd, wg, wu, wd, keep_up, keep_gate, hid0, hid1, by_gate, by_up, h1_out, a1t_out, a0t_out, h1, a1t, a0t, a0, a1, dy_ref, wd_v, send, recv, local, load, leave):
     me = lax.axis_index("dp")
     chip, core = me // 2, lax.rem(me, 2)
     ring = n // 2
@@ -38,11 +45,12 @@
 
     tokens, ff = hid0.shape
     d = x_ref.shape[1]
-    third = ff // 3
+    pieces = 6
+    piece = ff // pieces
     everything = (0, ff)
     units = [(sg, wg, 0, everything), (su, wu, 0, everything), (sd, wd, 0, (0, d)), (sd, wd, 1, (0, d))]
-    for t in range(3):
-        units += [(sg, wg, 1, (t * third, third)), (su, wu, 1, (t * third, third))]
+    for t in range(pieces):
+        units += [(sg, wg, 1, (t * piece, piece)), (su, wu, 1, (t * piece, piece))]
 
     def span(u, part):
         depth = units[u][0].shape[1]
@@ -133,11 +141,9 @@
             wg.at[0], wu.at[0], keep_up, keep_gate, hid0
         )
 
-    def last_layer(part, plan):
-        steps = third // bn
-
+    def last_layer(before, after):
         def body(g_ref, u_ref, d_ref, h_ref, bg_ref, bu_ref):
-            when(pl.program_id(0), plan)
+            when(pl.program_id(0), before)
             for r in range(0, tokens, sub):
                 here = pl.ds(r, sub)
                 gate = jnp.dot(a1[here, :], g_ref[...], preferred_element_type=F32)
@@ -148,11 +154,11 @@
                 h_ref[here, :] = (silu * up).astype(BF16)
                 bu_ref[here, :] = (by * silu).astype(BF16)
                 bg_ref[here, :] = (by * (up * (sig + silu * (1 - sig)))).astype(BF16)
-
-        w = pl.BlockSpec((d, bn), lambda j: (0, part * steps + j))
-        wt = pl.BlockSpec((bn, d), lambda j: (part * steps + j, 0))
-        tile = pl.BlockSpec((tokens, bn), lambda j: (0, part * steps + j))
-        pltpu.emit_pipeline(body, grid=(steps,), in_specs=[w, w, wt], out_specs=[tile] * 3)(
+            when(pl.program_id(0), after)
+
+        w, wt = pl.BlockSpec((d, bn), lambda j: (0, j)), pl.BlockSpec((bn, d), lambda j: (j, 0))
+        tile = pl.BlockSpec((tokens, bn), lambda j: (0, j))
+        pltpu.emit_pipeline(body, grid=(ff // bn,), in_specs=[w, w, wt], out_specs=[tile] * 3)(
             wg.at[1], wu.at[1], wd.at[1], hid1, by_gate, by_up
         )
 
@@ -166,7 +172,9 @@
             out = jnp.dot(hid_ref[...], wd_v[...], preferred_element_type=F32).astype(BF16)
             h = (x_ref[here, :].astype(F32) + out.astype(F32)).astype(BF16)
             h1[here, :] = h
-            a1[here, :] = normed(h)
+            a = normed(h)
+            a1[here, :] = a
+            a1t[:, here] = a.T
 
         pltpu.emit_pipeline(body, grid=(tokens // rm,), in_specs=[pl.BlockSpec((rm, ff), lambda i: (i, 0))], out_specs=[])(hid0)
 
@@ -179,49 +187,67 @@
 
     post(0)
     post(1)
+    get = pltpu.make_async_copy(dy, dy_ref, load)
+    get.start()
+    get.wait()
 
     @pl.loop(0, tokens // rm)
     def _(i):
         here = pl.ds(pl.multiple_of(i * rm, rm), rm)
-        a0[here, :] = normed(x_ref[here, :])
-
-    run((middle, 0), (relay, 0), (middle, 1), (post, 2), (relay, 1), (relay_far, 0), (relay_far, 1), (post, 3), (finish, 0), (finish, 1))()
-    pair = lambda p: lambda act: lambda: both(act, p)
-    p0, p1, p2 = pair(0), pair(1), pair(2)
-    first_layer(
-        {
-            6: run((middle, 2)),
-            11: run((relay, 2)),
-            12: p0(post),
-            16: run((middle, 3)),
-            21: run((relay, 3)),
-        }
-    )
-    run((relay_far, 2), (finish, 2))()
+        a = normed(x_ref[here, :])
+        a0[here, :] = a
+        a0t[:, here] = a.T
+
+    leaving = [pltpu.make_async_copy(one, out, leave.at[i]) for i, (one, out) in enumerate(((a0t, a0t_out), (h1, h1_out), (a1t, a1t_out)))]
+    leaving[0].start()
+
+    def on(p, *acts):
+        def act():
+            for f in acts:
+                both(f, p)
+
+        return act
+
+    run((middle, 0), (relay, 0), (middle, 1), (post, 2), (relay, 1), (relay_far, 0), (relay_far, 1), (finish, 0), (finish, 1))()
+
+    def first_piece():
+        middle(3)
+        on(0, post)()
+
+    first_layer({5: run((middle, 2), (post, 3)), 10: run((relay, 2)), 16: run((relay_far, 2)), 21: first_piece})
+    finish(2)
     get = pltpu.make_async_copy(wd.at[0], wd_v, load)
     get.start()
     get.wait()
 
-    def after_first():
-        p0(middle)()
-        p1(post)()
-
-    down({3: after_first, 6: p0(relay)})
-    run((relay_far, 3), (finish, 3))()
-    p0(relay_far)()
-    p0(finish)()
-
-    def after_second():
-        p1(middle)()
-        p2(post)()
-
-    last_layer(0, {2: after_second, 5: p1(relay)})
-    p1(relay_far)()
-    p1(finish)()
-    last_layer(1, {2: p2(middle), 5: p2(relay)})
-    p2(relay_far)()
-    p2(finish)()
-    last_layer(2, {})
+    def second_piece():
+        on(0, middle)()
+        on(1, post)()
+
+    down({0: run((relay, 3)), 4: run((relay_far, 3)), 7: second_piece})
+    finish(3)
+    on(0, relay, relay_far, finish)()
+    leaving[1].start()
+    leaving[2].start()
+    steps = piece // bn
+    before, after = {}, {}
+
+    def advance(p):
+        def act():
+            on(p, middle)()
+            if p + 1 < pieces:
+                on(p + 1, post)()
+
+        return act
+
+    for p in range(1, pieces):
+        before[steps * p - 4] = advance(p)
+        before[steps * p - 3] = on(p, relay)
+        before[steps * p - 2] = on(p, relay_far)
+        after[steps * p - 2] = on(p, finish)
+    last_layer(before, after)
+    for one in leaving:
+        one.wait()
     for u in range(len(units)):
         for kind in range(11):
             move(u, kind).wait_send()
@@ -234,29 +260,90 @@
     vmem, hbm = pl.BlockSpec(memory_space=pltpu.VMEM), pl.BlockSpec(memory_space=pl.ANY)
     s = jax.ShapeDtypeStruct
     wide, thin = s((tokens, ff), F32), s((tokens, ff), BF16)
-    units, kinds = 10, 11
+    units, kinds = 16, 11
     return pl.pallas_call(
         functools.partial(forward_kernel, n),
         out_shape=(
             s((layers, d, ff), BF16), s((layers, d, ff), BF16), s((layers, ff, d), BF16),
-            wide, wide, thin, thin, thin, thin, s((tokens, d), BF16), s((tokens, d), BF16),
+            wide, wide, thin, thin, thin, thin, s((tokens, d), BF16), s((d, tokens), BF16), s((d, tokens), BF16),
         ),
-        in_specs=[vmem] * 5,
-        out_specs=[hbm] * 9 + [vmem] * 2,
+        in_specs=[vmem] + [hbm] * 4,
+        out_specs=[hbm] * 12,
         scratch_shapes=[
+            pltpu.VMEM((tokens, d), BF16),
+            pltpu.VMEM((d, tokens), BF16),
+            pltpu.VMEM((d, tokens), BF16),
+            pltpu.VMEM((tokens, d), BF16),
+            pltpu.VMEM((tokens, d), BF16),
             pltpu.VMEM((tokens, d), BF16),
             pltpu.VMEM((ff, d), BF16),
             pltpu.SemaphoreType.DMA((units, kinds)),
             pltpu.SemaphoreType.DMA((units, kinds)),
             pltpu.SemaphoreType.DMA((units,)),
             pltpu.SemaphoreType.DMA,
+            pltpu.SemaphoreType.DMA((3,)),
         ],
         compiler_params=pltpu.CompilerParams(collective_id=0, has_side_effects=True, vmem_limit_bytes=63 * 1024 * 1024),
         name="forward",
     )(x, dy, sg, su, sd)
 
 
-def tail_kernel(n, by_ref, at_ref, wd, keep_up, keep_gate, out, bg, bu, term, there, own, hold, first, second, far_a, far_b, low, high, send, recv):
+def through_norm_kernel(h_ref, by_ref, wg, wu, by_gate, by_up, out, wg_v, wu_v, load):
+    tokens, _ = h_ref.shape
+    ff = by_gate.shape[1]
+    rm = 256
+    gets = [pltpu.make_async_copy(w.at[1], w_v, load.at[i]) for i, (w, w_v) in enumerate(((wg, wg_v), (wu, wu_v)))]
+    for get in gets:
+        get.start()
+    for get in gets:
+        get.wait()
+
+    def body(bg_ref, bu_ref):
+        here = pl.ds(pl.multiple_of(pl.program_id(0) * rm, rm), rm)
+        by_a = mm(bg_ref[...], wg_v[...], NT).astype(BF16).astype(F32) + mm(bu_ref[...], wu_v[...], NT).astype(BF16).astype(F32)
+        added = normed_back(h_ref[here, :], by_a.astype(BF16))
+        out[here, :] = (by_ref[here, :].astype(F32) + added.astype(F32)).astype(BF16)
+
+    rows = pl.BlockSpec((rm, ff), lambda i: (i, 0))
+    pltpu.emit_pipeline(body, grid=(tokens // rm,), in_specs=[rows, rows], out_specs=[])(by_gate, by_up)
+
+
+def through_norm(h, by_h, wg, wu, by_gate, by_up):
+    tokens, d = h.shape
+    ff = by_gate.shape[1]
+    vmem, hbm = pl.BlockSpec(memory_space=pltpu.VMEM), pl.BlockSpec(memory_space=pl.ANY)
+    return pl.pallas_call(
+        through_norm_kernel,
+        out_shape=jax.ShapeDtypeStruct((tokens, d), BF16),
+        in_specs=[vmem] * 2 + [hbm] * 4,
+        out_specs=vmem,
+        scratch_shapes=[pltpu.VMEM((d, ff), BF16)] * 2 + [pltpu.SemaphoreType.DMA((2,))],
+        compiler_params=pltpu.CompilerParams(vmem_limit_bytes=62 * 1024 * 1024),
+        cost_estimate=pl.CostEstimate(flops=4 * tokens * d * ff, bytes_accessed=4 * (tokens + d) * ff, transcendentals=0),
+        name="through_norm",
+    )(h, by_h, wg, wu, by_gate, by_up)
+
+
+def by_weight(a_t, by, start, size):
+    d, tokens = a_t.shape
+    bn = 1024
+
+    def kernel(a_ref, by_ref, out_ref):
+        out_ref[...] = jnp.dot(a_ref[...], by_ref[...], preferred_element_type=F32).astype(BF16)
+
+    return pl.pallas_call(
+        kernel,
+        out_shape=jax.ShapeDtypeStruct((d, size), BF16),
+        grid=(size // bn,),
+        in_specs=[pl.BlockSpec((d, tokens), lambda j: (0, 0)), pl.BlockSpec((tokens, bn), lambda j: (0, start // bn + j))],
+        out_specs=pl.BlockSpec((d, bn), lambda j: (0, j)),
+        compiler_params=pltpu.CompilerParams(vmem_limit_bytes=48 * 1024 * 1024),
+        cost_estimate=pl.CostEstimate(flops=2 * d * tokens * size, bytes_accessed=2 * (d + tokens) * size, transcendentals=0),
+        name="by_weight",
+    )(a_t, by)
+
+
+def tail_kernel(n, by_ref, at_ref, wd, keep_up, keep_gate, out_gate, out_up, bg, bu, term, there, own, hold, first, second, far_a, far_b, low, high, send, recv):
     me = lax.axis_index("dp")
     chip, core = me // 2, lax.rem(me, 2)
     ring = n // 2
@@ -326,9 +413,9 @@
         for kind in (3, 4, 5, 6):
             move(u, kind).wait_recv()
         columns = pl.ds(pl.multiple_of(u * bn, bn), bn)
-        for which in range(2):
+        for which, out in enumerate((out_gate, out_up)):
             total = own[u, which] + low[u, which].astype(F32) + high[u, which].astype(F32)
-            out[which, :, columns] = total.astype(BF16)
+            out[:, columns] = total.astype(BF16)
 
     bm, sub = tokens // 2, 256
 
@@ -382,7 +469,7 @@
             move(u, kind).wait_send()
 
 
-def tail(n, by_h, a, wd, keep_up, keep_gate):
+def tail(n, by_h, a_t, wd, keep_up, keep_gate):
     tokens, d = by_h.shape
     ff = keep_up.shape[1]
     depth, bn = d // n, 512
@@ -391,9 +478,9 @@
     block = (depth, bn)
     return pl.pallas_call(
         functools.partial(tail_kernel, n),
-        out_shape=jax.ShapeDtypeStruct((2, depth, ff), BF16),
+        out_shape=(jax.ShapeDtypeStruct((depth, ff), BF16),) * 2,
         in_specs=[vmem, vmem, hbm, hbm, hbm],
-        out_specs=vmem,
+        out_specs=(vmem, vmem),
         scratch_shapes=[
             pltpu.VMEM((tokens, bn), BF16),
             pltpu.VMEM((tokens, bn), BF16),
@@ -412,14 +499,7 @@
         ],
         compiler_params=pltpu.CompilerParams(collective_id=1, has_side_effects=True, vmem_limit_bytes=63 * 1024 * 1024),
         name="tail",
-    )(by_h, a.T, wd, keep_up, keep_gate)
-
-
-def normed_back(h, by_a):
-    wide, by = h.astype(F32), by_a.astype(F32)
-    scale = lax.rsqrt(jnp.mean(wide**2, -1, keepdims=True) + 1e-6)
-    along = jnp.mean(by * wide, -1, keepdims=True)
-    return (by * scale - scale**3 * along * wide).astype(BF16)
+    )(by_h, a_t, wd, keep_up, keep_gate)
 
 
 def adamw(w, m, v, g):
@@ -438,23 +518,23 @@
     def inner(x, dy, *arrays):
         weights, m, v = (arrays[i : i + 3] for i in (0, 3, 6))
         layers = weights[0].shape[0]
-        wg, wu, wd, keep_up, keep_gate, hid0, hid1, by_gate, by_up, h1, a1 = forward(n, x[0], dy[0], *weights)
-        a0, by_h = normed(x[0]), dy[0]
+        wg, wu, wd, keep_up, keep_gate, hid0, hid1, by_gate, by_up, h1, a1t, a0t = forward(n, x[0], dy[0], *weights)
+        by_h = dy[0]
+        ff = by_gate.shape[1]
+        g_gate = by_weight(a1t, by_gate, 0, ff)
+        r1 = scatter(g_gate)
+        hid1, g_gate = lax.optimization_barrier((hid1, g_gate))
         g_down = mm(hid1, by_h, TN).astype(BF16)
         r0 = scatter(g_down)
-        by_gate, by_up, g_down = lax.optimization_barrier((by_gate, by_up, g_down))
-        g_gate = mm(a1, by_gate, TN).astype(BF16)
-        r1 = scatter(g_gate)
-        by_up, g_gate = lax.optimization_barrier((by_up, g_gate))
-        g_up = mm(a1, by_up, TN).astype(BF16)
+        by_up, g_down = lax.optimization_barrier((by_up, g_down))
+        g_up = by_weight(a1t, by_up, 0, ff)
         r2 = scatter(g_up)
         by_gate, by_up, g_up = lax.optimization_barrier((by_gate, by_up, g_up))
-        by_a = mm(by_gate, wg[1], NT).astype(BF16) + mm(by_up, wu[1], NT).astype(BF16)
-        by_h = by_h + normed_back(h1, by_a)
+        by_h = through_norm(h1, by_h, wg, wu, by_gate, by_up)
         g_down = mm(hid0, by_h, TN).astype(BF16)
         r3 = scatter(g_down)
         by_h, g_down = lax.optimization_barrier((by_h, g_down))
-        r4, r5 = tail(n, by_h, a0, wd, keep_up, keep_gate)
+        r4, r5 = tail(n, by_h, a0t, wd, keep_up, keep_gate)
         mine = [[r4, r5, r3], [r1, r2, r0]]
         new = []
         for i in range(3):

time: 758 us -> 606 us (0.80)
  waiting for transfers between devices: 129 us -> 1.69 us
  matrix products: 159 us -> 54.1 us
  Pallas kernels: 408 us -> 498 us
    reduce_scatter x4, waiting for transfers between devices: 127 us -> 0.81 us  [scatter(): return lax.psum_scatter(g, 'dp', scatter_dimension=0, tiled=True)]
    pallas_call x1 -> x4, Pallas kernels: 130 us -> 235 us  [the longest x1 129 us: tail(): pl.pallas_call(functools.partial(tail_kernel, n), out_shape=(jax.ShapeDty...]
    dot_general x6 -> x2, matrix products: 159 us -> 54.1 us  [mm(): return lax.dot_general(a, w, (dims, ((), ())), preferred_element_type=F32)]
    pallas_call x1, Pallas kernels: 278 us -> 264 us  [forward(): pl.pallas_call(functools.partial(forward_kernel, n), out_shape=(s((layers...]
  transfers between devices with their start and end apart: 4 -> 4, of which waited for: 3 -> 1; matrix products, arithmetic and copies ran while one was open for 4% -> 12% of each run, Pallas kernels for 17% -> 35%
where the time goes in v2:
time: 606 us; the launch traced here: 597 us
  Pallas kernels  498 us (82%)
  matrix products  54.1 us (9%)
  other arithmetic  26.7 us (4%)
  between operations  14.1 us (2%)
    pallas_call x1, Pallas kernels, forward(): pl.pallas_call(functools.partial(forward_kernel, n), out_shape=(s((layers...  264 us
    pallas_call x1, Pallas kernels, tail(): pl.pallas_call(functools.partial(tail_kernel, n), out_shape=(jax.ShapeDty...  129 us
    pallas_call x1, Pallas kernels, through_norm(): pl.pallas_call(through_norm_kernel, out_shape=jax.ShapeDtypeStruct((token...  57.5 us
    dot_general x2, matrix products, mm(): return lax.dot_general(a, w, (dims, ((), ())), preferred_element_type=F32)  54.1 us
    pallas_call x2, Pallas kernels, by_weight(): pl.pallas_call(kernel, out_shape=jax.ShapeDtypeStruct((d, size), BF16), g...  47.9 us
    convert_element_type x3, other arithmetic, adamw(): return ((w - 0.02 * step).astype(BF16), m, v)  26.7 us
  transfers between devices with their start and end apart: 4, of which 1 were waited for; matrix products, arithmetic and copies ran while one was open for 12% of the time, Pallas kernels for 35%

profile of v2, /device:TPU:112, one launch (start us, length us, event | category | flops | bytes accessed | tf_op | source)
XLA Modules:
  0.0 597.1 jit_solution(7395191317323424088)
XLA Ops:
  7.2 0.1 reduce-scatter.5.cloned.1.call-start
  7.3 263.5 %forward.1 = (bf16[2,768,6144]{2,1,0:T(8,128)(2,1)}, bf16[2,768,6144]{2,1,0:T(8,128)(2,1)}, bf16[2,6144,768]{2,1,0:T(8,128)(2,1)}, f32[2048,6144]{1,0:T(8,128)},...) custom-call(bf16[2048,768]{1,0:T(8,128)(2,1)} %bitcast.13, ...), custom_call_target="tpu_custom_call" | custom-call | tf_op jit(solution)/shard_map/forward/pallas_call | solution.py:264
  270.8 0.0 copy-start
  270.8 1.9 copy-done
  272.7 23.9 %by_weight.2 = bf16[768,6144]{1,0:T(8,128)(2,1)} custom-call(bf16[768,2048]{1,0:T(8,128)(2,1)S(1)} %copy-done, bf16[2048,6144]{1,0:T(8,128)(2,1)} %get-tuple-element.37.by_ref.by_gate), custom_call_target="tpu_custom_call" | custom-call | flops 19327352832 | bytes 34603008 | tf_op jit(solution)/shard_map/by_weight/pallas_call | solution.py:334
  296.6 0.1 reduce-scatter.5.cloned.1.call-update
  296.6 0.1 reduce-scatter.7.cloned.1.call-start
  296.7 0.0 copy-start.1
  296.7 27.4 %convolution_convert_fusion.1 = bf16[6144,768]{1,0:T(8,128)(2,1)} fusion(bf16[2048,6144]{1,0:T(8,128)(2,1)} %get-tuple-element.35, bf16[1,2048,768]{2,1,0:T(8,128)(2,1)} %param.12), kind=kOutput, calls=%fused_computation.1 | convolution fusion | flops 19332071424 | bytes 37748736 | tf_op jit(solution)/shard_map/dot_general | solution.py:17
  324.1 0.0 copy-done.1
  324.1 24.0 %by_weight.3 = bf16[768,6144]{1,0:T(8,128)(2,1)} custom-call(bf16[768,2048]{1,0:T(8,128)(2,1)S(1)} %copy-done.1, bf16[2048,6144]{1,0:T(8,128)(2,1)} %get-tuple-element.38.by_ref.by_up), custom_call_target="tpu_custom_call" | custom-call | flops 19327352832 | bytes 34603008 | tf_op jit(solution)/shard_map/by_weight/pallas_call | solution.py:334
  348.1 0.1 reduce-scatter.7.cloned.1.call-update
  348.2 0.1 reduce-scatter.11.cloned.1.call-start
  348.3 0.7 reduce-scatter.11.cloned.1.call-update
  349.0 0.1 reduce-scatter.9.cloned.1.call-start
  349.1 57.5 %through_norm.1.by_ref = bf16[2048,768]{1,0:T(8,128)(2,1)} custom-call(bf16[2048,768]{1,0:T(8,128)(2,1)} %get-tuple-element.28.h_ref, bf16[2048,768]{1,0:T(8,128)(2,1)} %bitcast.15, bf16[2,768,6144]{2,1,0:T(8,128)(2,1)} %get-tuple-element.29.wg, bf16[2,768,6144]{2,1,0:T(8,128)(2,1)} %get-tuple-element.30.wu, ...), custom_call_target="tpu_custom_call" | custom-call | flops 38654705664 | bytes 69206016 | tf_op jit(solution)/shard_map/through_norm/pallas_call | solution.py:315
  406.6 26.7 %convolution_convert_fusion = bf16[6144,768]{1,0:T(8,128)(2,1)} fusion(bf16[2048,6144]{1,0:T(8,128)(2,1)} %get-tuple-element.39, bf16[2048,768]{1,0:T(8,128)(2,1)} %through_norm.1.by_ref), kind=kOutput, calls=%fused_computation | convolution fusion | flops 19332071424 | bytes 37748736 | tf_op jit(solution)/shard_map/dot_general | solution.py:17
  433.3 0.1 reduce-scatter.9.cloned.1.call-update
  433.4 129.4 %tail.1 = (bf16[96,6144]{1,0:T(8,128)(2,1)}, bf16[96,6144]{1,0:T(8,128)(2,1)}) custom-call(bf16[2048,768]{1,0:T(8,128)(2,1)} %through_norm.1.by_ref, bf16[768,2048]{1,0:T(8,128)(2,1)} %get-tuple-element.41.at_ref, bf16[2,6144,768]{2,1,0:T(8,128)(2,1)} %get-tuple-element.42.wd, f32[2048,6144]{1,0:T(8,128)} %get-tuple-element.43.keep_up, ...), custom_call_target="tpu_custom_call" | custom-call | tf_op jit(solution)/shard_map/tail/pallas_call | solution.py:479
  562.7 0.0 reduce-scatter.5.cloned.1.call-done
  562.8 0.0 copy-start.2
  562.8 0.0 copy-start.3
  562.8 9.5 %fusion.2 = (bf16[2,96,6144]{2,1,0:T(8,128)(2,1)}, f32[2,96,6144]{2,1,0:T(8,128)}, f32[2,96,6144]{2,1,0:T(8,128)}) fusion(bf16[2,96,6144]{2,1,0:T(8,128)(2,1)} %sg.1, bf16[1,96,6144]{2,1,0:T(8,128)(2,1)} %bitcast.17, bf16[1,96,6144]{2,1,0:T(8,128)(2,1)} %bitcast.21, f32[2,96,6144]{2,1,0:T(8,128)} %param.19, f32[2,96,6144]{2,1,0:T(8,128)} %param.16), kind=kLoop, calls=%fused_computation.16 | loop fusion | flops 22413312 | bytes 25952256 | tf_op jit(solution)/shard_map/convert_element_type | solution.py:509
  572.3 0.0 reduce-scatter.7.cloned.1.call-done
  572.3 0.0 copy-done.2
  572.3 0.0 copy-done.3
  572.3 8.3 %fusion.6 = (bf16[2,96,6144]{2,1,0:T(8,128)(2,1)}, f32[2,96,6144]{2,1,0:T(8,128)}, f32[2,96,6144]{2,1,0:T(8,128)}) fusion(bf16[2,96,6144]{2,1,0:T(8,128)(2,1)S(1)} %copy-done.2, bf16[1,96,6144]{2,1,0:T(8,128)(2,1)} %bitcast.18, bf16[1,96,6144]{2,1,0:T(8,128)(2,1)S(1)} %bitcast.20, f32[2,96,6144]{2,1,0:T(8,128)} %param.20, f32[2,96,6144]{2,1,0:T(8,128)} %param.17), kind=kLoop, calls=%fused_computation.20 | loop fusion | flops 22413312 | bytes 25952256 | tf_op jit(solution)/shard_map/convert_element_type | solution.py:509
  580.6 0.0 reduce-scatter.11.cloned.1.call-done
  580.6 0.8 reduce-scatter.9.cloned.1.call-done
  581.4 8.9 %fusion.10 = (bf16[2,768,768]{2,1,0:T(8,128)(2,1)}, f32[2,768,768]{2,1,0:T(8,128)}, f32[2,768,768]{2,1,0:T(8,128)}) fusion(bf16[2,768,768]{2,1,0:T(8,128)(2,1)} %sd.1, bf16[1,768,768]{2,1,0:T(8,128)(2,1)} %bitcast.16, bf16[1,768,768]{2,1,0:T(8,128)(2,1)} %bitcast.19, f32[2,768,768]{2,1,0:T(8,128)} %param.21, f32[2,768,768]{2,1,0:T(8,128)} %param.18), kind=kLoop, calls=%fused_computation.24 | loop fusion | flops 22413312 | bytes 25952256 | tf_op jit(solution)/shard_map/convert_element_type | solution.py:509
Async XLA Ops:
  7.2 555.6 %reduce-scatter.5.cloned.1.call-start = ((), (), s32[]{:S(2)}) async-start(), calls=%async_computation.4 | async-start | bytes 10616832 | tf_op jit(solution)/shard_map/reduce_scatter | solution.py:516
  270.8 1.9 copy-start
  296.6 275.7 %reduce-scatter.7.cloned.1.call-start = ((), (), s32[]{:S(2)}) async-start(), calls=%async_computation.5 | async-start | bytes 10616832 | tf_op jit(solution)/shard_map/reduce_scatter | solution.py:516
  296.7 27.4 %copy-start.1 = (bf16[768,2048]{1,0:T(8,128)(2,1)S(1)}, bf16[768,2048]{1,0:T(8,128)(2,1)}, u32[]{:S(2)}) copy-start(bf16[768,2048]{1,0:T(8,128)(2,1)} %get-tuple-element.34.a_ref) | copy-start | bytes 9437188
  348.2 232.4 %reduce-scatter.11.cloned.1.call-start = ((), (), s32[]{:S(2)}) async-start(), calls=%async_computation.7 | async-start | bytes 10616832 | tf_op jit(solution)/shard_map/reduce_scatter | solution.py:516
  349.0 232.4 %reduce-scatter.9.cloned.1.call-start = ((), (), s32[]{:S(2)}) async-start(), calls=%async_computation.6 | async-start | bytes 10616832 | tf_op jit(solution)/shard_map/reduce_scatter | solution.py:516
  562.8 9.5 %copy-start.2 = (bf16[2,96,6144]{2,1,0:T(8,128)(2,1)S(1)}, bf16[2,96,6144]{2,1,0:T(8,128)(2,1)}, u32[]{:S(2)}) copy-start(bf16[2,96,6144]{2,1,0:T(8,128)(2,1)} %su.1) | copy-start | bytes 7077892
  562.8 9.5 %copy-start.3 = (bf16[96,6144]{1,0:T(8,128)(2,1)S(1)}, bf16[96,6144]{1,0:T(8,128)(2,1)}, u32[]{:S(2)}) copy-start(bf16[96,6144]{1,0:T(8,128)(2,1)} %get-tuple-element.46) | copy-start | bytes 3538948
Sparse Core Ops, SparseCore 0:
  296.8 53.9 reduce-scatter.4
  353.0 52.9 reduce-scatter.6
  408.3 70.5 reduce-scatter.10
  481.1 100.2 reduce-scatter.8
